TPU v7x, 32 devices: a whole 2x2x4 slice. The times are simulated.
32 devices in a mesh: seq: 16 (over z, y, core), mp: 2 (over x).
Axes of the slice: x: 2, y: 2, z: 4, core: 2. Of those that a mesh axis runs over, the one named last changes fastest.
Arguments:
- query: bfloat16 [4096, 3072], P('seq', 'mp'), may hold values from -4.5 to 4.5
- key: bfloat16 [4096, 3072], P('seq', 'mp'), may hold values from -4.5 to 4.5
- value: bfloat16 [4096, 3072], P('seq', 'mp'), may hold values from -6 to 6
- clip_lengths: int32 [4, 4], replicated, may hold values from 0 to 1024, as said below
Outputs:
- attended: bfloat16 [4096, 3072], P(('seq', 'mp'))
Inputs may be any that keep to these rules, and one draw needn't show every extreme that they name: `clip_lengths`: each row sums to 1024; a clip slot may be empty; in some bucket one clip fills all 1024 tokens.
All inputs are finite; a program needn't handle non-finite values.
Results may differ from a plain program's by a relative error of at most 0.01.
Values may be sent and summed in bfloat16 or wider, within the bound.
A program may use at most 64 MiB of HBM per device.

v0:
```python
import functools

import jax
import jax.numpy as jnp
from jax import lax
from jax.experimental import pallas as pl
from jax.experimental.pallas import tpu as pltpu
from jax.sharding import PartitionSpec as P

HD = 128
NEG = -1e30
LOG2E = 1.4426950408889634
MESH = pl.DeviceIdType.MESH


def kernel(
    group, pair, mp, heads, lead,
    lengths, query, key, value, out,
    q_buf, k_buf, v_buf, o_buf, first, p_buf, t_buf,
    q_in, k_in, v_in, o_in, q_out, k_out, v_out, o_out, first_in, ready,
):
    rows = query.shape[0]
    part = rows // mp
    per_core = heads // pair
    others = group // pair
    extra = lead * (others - 1)
    held = per_core - extra
    slots = lengths.shape[1]
    seq_index = lax.axis_index("seq")
    mp_index = lax.axis_index("mp")
    bucket = seq_index // group
    place = lax.rem(seq_index, group)
    core = lax.rem(place, pair)
    chip = place // pair

    def chip_at(chip_step):
        return lax.rem(chip + chip_step, others)

    def seq_of(chip_step, there_core):
        return bucket * group + chip_at(chip_step) * pair + there_core

    def head_of(slot, there_chip):
        if isinstance(slot, int) and slot < lead:
            return slot * others + there_chip
        return slot + extra

    def columns(owner, head):
        return pl.ds(pl.multiple_of((owner * per_core + head) * HD, HD), HD)

    def block_at(index):
        return pl.ds(pl.multiple_of(index * rows, rows), rows)

    kinds = ((query, q_buf, q_out, q_in), (key, k_buf, k_out, k_in), (value, v_buf, v_out, v_in))

    def local_copies(slot):
        mine = columns(core, head_of(slot, chip))
        return [
            pltpu.make_async_copy(source.at[:, mine], buf.at[slot, block_at(place), :], landed.at[slot, place])
            for source, buf, left, landed in kinds
        ]

    def far_kinds(slot):
        whole = isinstance(slot, int) and slot < lead
        return (0, 1, 2) if whole else (1, 2)

    far = [(chip_step, there_core) for there_core in range(pair) for chip_step in range(1, others)]

    def first_copies():
        return [
            pltpu.make_async_copy(
                kinds[kind][0].at[:, columns(there_core, head_of(0, chip_at(chip_step)))],
                first.at[kind, chip_step * pair + there_core],
                first_in.at[kind, chip_step * pair + there_core],
            )
            for kind in far_kinds(0) for chip_step, there_core in far
        ]

    def send(slot, chip_step, there_core, kind, staged=False):
        source, buf, left, landed = kinds[kind]
        index = chip_step * pair + there_core
        if staged:
            origin = first.at[kind, index]
        else:
            origin = source.at[:, columns(there_core, head_of(slot, chip_at(chip_step)))]
        return pltpu.make_async_remote_copy(
            src_ref=origin, dst_ref=buf.at[slot, block_at(place), :],
            send_sem=left.at[slot, index], recv_sem=landed.at[slot, place],
            device_id={"seq": seq_of(chip_step, there_core), "mp": mp_index}, device_id_type=MESH,
        )

    def far_sends(slot, staged=False):
        return [send(slot, a, b, kind, staged) for kind in far_kinds(slot) for a, b in far]

    def near_sends(slot):
        return [
            send(slot, 0, lax.rem(core + step, pair), kind)
            for kind in range(3) for step in range(1, pair)
        ]

    def result(turn, slot, chip_step, core_step, mp_step):
        there_core = lax.rem(core + core_step, pair)
        there_mp = lax.rem(mp_index + mp_step, mp)
        source = o_buf.at[turn, pl.ds(pl.multiple_of(there_core * rows + there_mp * part, part), part), :]
        column = (mp_index * heads + core * per_core + head_of(slot, chip)) * HD
        target = out.at[:, pl.ds(pl.multiple_of(column, HD), HD)]
        index = core_step * mp + mp_step
        if chip_step == 0 and index == 0:
            return pltpu.make_async_copy(source, target, o_in.at[turn, index])
        return pltpu.make_async_remote_copy(
            src_ref=source, dst_ref=target, send_sem=o_out.at[turn, index], recv_sem=o_in.at[turn, index],
            device_id={"seq": seq_of(chip_step, there_core), "mp": there_mp}, device_id_type=MESH,
        )

    for copy in first_copies():
        copy.start()

    barrier = pltpu.get_barrier_semaphore()
    beside = [(seq_of(0, b), lax.rem(mp_index + m, mp)) for b in range(pair) for m in range(1, mp)]
    greeted = [(seq_of(a, b), mp_index) for a, b in far]
    greeted += [(seq_of(0, lax.rem(core + b, pair)), mp_index) for b in range(1, pair)]
    greeted += beside
    for there_seq, there_mp in greeted:
        pl.semaphore_signal(
            barrier, inc=1, device_id={"seq": there_seq, "mp": there_mp}, device_id_type=MESH
        )

    for slot in range(max(lead, 1)):
        for copy in local_copies(slot):
            copy.start()

    @pl.loop(max(lead, 1), held)
    def _(slot):
        for copy in local_copies(slot):
            copy.start()

    ends = []
    running = jnp.int32(0)
    for i in range(slots):
        running = running + lengths[bucket, i]
        ends.append(running)

    def ids(offset):
        found = jnp.zeros_like(offset)
        for end in ends:
            found = found + (offset >= end).astype(jnp.int32)
        return found

    k_ids = ids(lax.broadcasted_iota(jnp.int32, (1, group * rows), 1))

    for copy in first_copies():
        copy.wait()
    pl.semaphore_wait(barrier, len(greeted))

    for slot in range(max(lead, 1)):
        for copy in far_sends(slot, slot == 0) + near_sends(slot):
            copy.start()

    @pl.loop(max(lead, 1), held)
    def _(slot):
        for copy in far_sends(slot) + near_sends(slot):
            copy.start()

    if lead:
        for there_seq, there_mp in beside:
            pl.semaphore_signal(
                ready, inc=1, device_id={"seq": there_seq, "mp": there_mp}, device_id_type=MESH
            )

    def arrived(kind, slot, base, count):
        buf, landed = kinds[kind][1], kinds[kind][3]
        for i in range(count):
            ref = buf.at[slot, block_at(base + i), :]
            pltpu.make_async_copy(ref, ref, landed.at[slot, base + i]).wait()

    factor = LOG2E / HD**0.5

    def weigh(slot, chip_step):
        keys = k_buf[slot]
        for b in range(pair):
            block = pl.ds(b * rows, rows)
            from_row = (chip_at(chip_step) * pair + b) * rows
            q_ids = ids(lax.broadcasted_iota(jnp.int32, (rows, 1), 0) + from_row)
            score = lax.dot_general(
                q_buf[slot, pl.ds(pl.multiple_of(from_row, rows), rows), :], keys,
                (((1,), (1,)), ((), ())), preferred_element_type=jnp.float32,
            )
            score = jnp.where(q_ids == k_ids, score, NEG)
            top = jnp.max(score, axis=1, keepdims=True)
            weight = jnp.exp2((score - top) * factor)
            t_buf[block, :] = jnp.broadcast_to(jnp.sum(weight, axis=1, keepdims=True), (rows, HD))
            p_buf[block, :] = weight.astype(jnp.bfloat16)

    def attend(turn, slot, chip_step):
        for core_step in reversed(range(pair)):
            block = block_at(lax.rem(core + core_step, pair))
            summed = jnp.dot(p_buf[block, :], v_buf[slot], preferred_element_type=jnp.float32)
            o_buf[turn, block, :] = (summed / t_buf[block, :]).astype(jnp.bfloat16)
            if chip_step == 0:
                for mp_step in reversed(range(mp)):
                    result(turn, slot, 0, core_step, mp_step).start()

    def far_results(mp_steps):
        return [
            result(slot * (others - 1) + a - 1, slot, a, core_step, mp_step)
            for slot in range(lead) for mp_step in mp_steps
            for core_step in range(pair) for a in range(1, others)
        ]

    def settle(turn, slot, chip_step=0):
        for core_step in range(pair):
            for mp_step in range(mp):
                copy = result(turn, slot, chip_step, core_step, mp_step)
                if chip_step == 0 and core_step == 0 and mp_step == 0:
                    copy.wait()
                else:
                    copy.wait_send()
                    copy.wait_recv()

    for slot in range(lead):
        arrived(0, slot, 0, group)
        arrived(1, slot, 0, group)
        for step in range(1, others):
            weigh(slot, step)
            if step == 1:
                arrived(2, slot, 0, group)
            attend(slot * (others - 1) + step - 1, slot, step)
        weigh(slot, 0)
        attend(slot + extra, slot, 0)
        for copy in far_sends(slot, slot == 0) + near_sends(slot):
            copy.wait_send()
    if lead:
        pl.semaphore_wait(ready, len(beside))
        for copy in far_results(list(range(1, mp)) + [0]):
            copy.start()

    @pl.loop(lead, held)
    def _(slot):
        arrived(0, slot, chip * pair, pair)
        arrived(1, slot, 0, group)
        weigh(slot, 0)
        arrived(2, slot, 0, group)
        attend(slot + extra, slot, 0)
        for copy in far_sends(slot) + near_sends(slot):
            copy.wait_send()

        @pl.when(slot > lead)
        def _():
            settle(slot + extra - 1, slot - 1)

    for slot in range(lead):
        settle(slot + extra, slot)
    settle(held - 1 + extra, held - 1)
    for slot in range(lead):
        for step in range(1, others):
            settle(slot * (others - 1) + step - 1, slot, step)


def shards(query, key, value, clip_lengths):
    rows, width = query.shape
    heads = width // HD
    group = lax.axis_size("seq") // clip_lengths.shape[0]
    mp = lax.axis_size("mp")
    pair = 2 if group % 2 == 0 and heads % 2 == 0 else 1
    per_core = heads // pair
    others = group // pair
    lead = min(2, (per_core - 1) // others) if others > 1 else 0
    held = per_core - lead * (others - 1)
    dma = pltpu.SemaphoreType.DMA
    whole = pl.BlockSpec(memory_space=pl.ANY)
    return pl.pallas_call(
        functools.partial(kernel, group, pair, mp, heads, lead),
        out_shape=pltpu.VMEM((rows // mp, width * mp), jnp.bfloat16),
        in_specs=[pl.BlockSpec(memory_space=pltpu.SMEM), whole, whole, whole],
        out_specs=pl.BlockSpec(memory_space=pltpu.VMEM),
        scratch_shapes=[
            pltpu.VMEM((held, group * rows, HD), jnp.bfloat16),
            pltpu.VMEM((held, group * rows, HD), jnp.bfloat16),
            pltpu.VMEM((held, group * rows, HD), jnp.bfloat16),
            pltpu.VMEM((per_core, pair * rows, HD), jnp.bfloat16),
            pltpu.VMEM((3, group, rows, HD), jnp.bfloat16),
            pltpu.VMEM((pair * rows, group * rows), jnp.bfloat16),
            pltpu.VMEM((pair * rows, HD), jnp.float32),
            dma((held, group)), dma((held, group)), dma((held, group)), dma((per_core, pair * mp)),
            dma((held, group)), dma((held, group)), dma((held, group)), dma((per_core, pair * mp)),
            dma((3, group)), pltpu.SemaphoreType.REGULAR,
        ],
        compiler_params=pltpu.CompilerParams(collective_id=0, has_side_effects=True),
        name="packed_attention",
    )(clip_lengths, query, key, value)


def solution(mesh):
    in_specs = (P("seq", "mp"), P("seq", "mp"), P("seq", "mp"), P())
    out_specs = P(("seq", "mp"), None)
    return jax.shard_map(shards, mesh=mesh, in_specs=in_specs, out_specs=out_specs, check_vma=False)
```

profile of v0, /device:TPU:0, one launch (start us, length us, event | category | flops | bytes accessed | tf_op | source)
XLA Modules:
  0.0 42.4 jit_solution(7805610679569305266)
XLA Ops:
  0.0 41.5 %packed_attention.1 = bf16[128,3072]{1,0:T(8,128)(2,1)S(1)} custom-call(s32[4,4]{1,0:T(4,128)} %lengths.1, bf16[256,1536]{1,0:T(8,128)(2,1)} %query.1, bf16[256,1536]{1,0:T(8,128)(2,1)} %key.1, bf16[256,1536]{1,0:T(8,128)(2,1)} %value.1), custom_call_target="tpu_custom_call" | custom-call | tf_op jit(solution)/shard_map/packed_attention/pallas_call | solution.py:270
  41.6 0.9 %copy.6 = bf16[128,3072]{1,0:T(8,128)(2,1)} copy(bf16[128,3072]{1,0:T(8,128)(2,1)S(1)} %packed_attention.1) | data formatting | bytes 1572864
where the time goes:
time: 42.6 us; the launch traced here: 42.4 us
  Pallas kernels  41.5 us (97%)
  local copies, waits for them, and re-layouts  0.88 us (2%)
    pallas_call x1, Pallas kernels, shards(): pl.pallas_call(functools.partial(kernel, group, pair, mp, heads, lead), o...  41.5 us
    unnamed x1, local copies, waits for them, and re-layouts  0.88 us

commit v1 on v0

--- a/solution.py
+++ b/solution.py
@@ -255,11 +255,223 @@
             settle(slot * (others - 1) + step - 1, slot, step)
 
 
+def duo(
+    heads,
+    lengths, query, key, value, out,
+    kept, weights, totals, results, table,
+    landed, sent, result_in, result_out, table_in, ready,
+):
+    rows = query.shape[0]
+    mp = lax.axis_size("mp")
+    part = rows // mp
+    per_core = heads // 2
+    wide = per_core // 3
+    width = wide * HD
+    slots = lengths.shape[1]
+    seq_index = lax.axis_index("seq")
+    mp_index = lax.axis_index("mp")
+    bucket = seq_index // 4
+    place = lax.rem(seq_index, 4)
+    core = lax.rem(place, 2)
+    chip = place // 2
+    other = 1 - chip
+    inputs = (query, key, value)
+
+    def device(there_chip, there_core, there_mp):
+        return {"seq": bucket * 4 + there_chip * 2 + there_core, "mp": there_mp}
+
+    def columns(owner, third):
+        return pl.ds(pl.multiple_of(owner * per_core * HD + third * width, width), width)
+
+    def block_at(index):
+        return pl.ds(pl.multiple_of(index * rows, rows), rows)
+
+    def send(kind, phase, there_chip, there_core):
+        third = 2 if phase else there_chip
+        return pltpu.make_async_remote_copy(
+            src_ref=inputs[kind].at[:, columns(there_core, third)],
+            dst_ref=kept.at[kind, phase, block_at(place), :],
+            send_sem=sent, recv_sem=landed.at[kind, phase],
+            device_id=device(there_chip, there_core, mp_index), device_id_type=MESH,
+        )
+
+    def keep(kind, phase):
+        third = 2 if phase else chip
+        return pltpu.make_async_copy(
+            inputs[kind].at[:, columns(core, third)], kept.at[kind, phase, block_at(place), :], landed.at[kind, phase]
+        )
+
+    def result(turn, there_chip, core_step, mp_step):
+        there_core = lax.rem(core + core_step, 2)
+        there_mp = lax.rem(mp_index + mp_step, mp)
+        first = (there_chip * 2 + there_core) * rows + there_mp * part
+        source = results.at[turn, pl.ds(pl.multiple_of(first, part), part), :]
+        third = 2 if turn else chip
+        column = (mp_index * heads + core * per_core) * HD + third * width
+        target = out.at[:, pl.ds(pl.multiple_of(column, width), width)]
+        if there_chip is chip and core_step == 0 and mp_step == 0:
+            target[...] = source[...]
+            return
+        pltpu.make_async_remote_copy(
+            src_ref=source, dst_ref=target, send_sem=result_out, recv_sem=result_in,
+            device_id=device(there_chip, there_core, there_mp), device_id_type=MESH,
+        ).start()
+
+    barrier = pltpu.get_barrier_semaphore()
+    far = [device(other, b, mp_index) for b in range(2)]
+    beside = [device(chip, b, lax.rem(mp_index + m, mp)) for m in range(1, mp) for b in range(2)]
+
+    def greet(semaphore, devices):
+        for there in devices:
+            pl.semaphore_signal(semaphore, inc=1, device_id=there, device_id_type=MESH)
+
+    greet(barrier, far)
+    pl.when(chip == 0)(lambda: greet(barrier, beside))
+    known = len(far) + lax.select(chip == 0, len(beside), 0)
+    pl.semaphore_wait(barrier, known)
+
+    for kind, phase in ((1, 0), (0, 0), (2, 0), (1, 1), (2, 1)):
+        for there_core in range(2):
+            send(kind, phase, other, there_core).start()
+    fetch = pltpu.make_async_copy(lengths, table, table_in)
+    fetch.start()
+    for phase in range(2):
+        for kind in (1, 0, 2):
+            keep(kind, phase).start()
+
+    greet(ready, far)
+
+    @pl.when(chip == 0)
+    def _():
+        greet(ready, beside)
+        pl.semaphore_wait(ready, len(far) + len(beside))
+        greet(ready, far)
+
+    pl.when(chip != 0)(lambda: pl.semaphore_wait(ready, 2 * len(far)))
+
+    for phase in range(2):
+        for kind in (1, 0, 2):
+            send(kind, phase, chip, 1 - core).start()
+
+    fetch.wait()
+    ends = []
+    running = jnp.int32(0)
+    for i in range(slots):
+        running = running + table[bucket, i]
+        ends.append(running)
+
+    def ids(offset):
+        found = jnp.zeros_like(offset)
+        for end in ends:
+            found = found + (offset >= end).astype(jnp.int32)
+        return found
+
+    k_ids = ids(lax.broadcasted_iota(jnp.int32, (1, 4 * rows), 1))
+    factor = LOG2E / HD**0.5
+
+    def arrived(kind, phase):
+        ref = kept.at[kind, phase]
+        if kind == 0 and phase:
+            ref = kept.at[kind, phase, pl.ds(pl.multiple_of(chip * 2 * rows, rows), 2 * rows), :]
+        pltpu.make_async_copy(ref, ref, landed.at[kind, phase]).wait()
+
+    def weigh(phase, index):
+        block = block_at(index)
+        q_ids = ids(lax.broadcasted_iota(jnp.int32, (rows, 1), 0) + index * rows)
+        for head in range(wide):
+            lanes = slice(head * HD, (head + 1) * HD)
+            score = lax.dot_general(
+                kept[0, phase, block, lanes], kept[1, phase, :, lanes],
+                (((1,), (1,)), ((), ())), preferred_element_type=jnp.float32,
+            )
+            score = jnp.where(q_ids == k_ids, score, NEG)
+            top = jnp.max(score, axis=1, keepdims=True)
+            weight = jnp.exp2((score - top) * factor)
+            totals[head, block, :] = jnp.broadcast_to(jnp.sum(weight, axis=1, keepdims=True), (rows, HD))
+            weights[head, block, :] = weight.astype(jnp.bfloat16)
+
+    def attend(phase, index):
+        block = block_at(index)
+        for head in range(wide):
+            lanes = slice(head * HD, (head + 1) * HD)
+            summed = jnp.dot(weights[head, block, :], kept[2, phase, :, lanes], preferred_element_type=jnp.float32)
+            results[phase, block, lanes] = (summed / totals[head, block, :]).astype(jnp.bfloat16)
+
+    arrived(1, 0)
+    arrived(0, 0)
+
+    @pl.loop(0, 4)
+    def _(step):
+        weigh(0, lax.rem(other * 2 + step, 4))
+
+    arrived(2, 0)
+
+    @pl.loop(0, 4)
+    def _(step):
+        attend(0, lax.rem(other * 2 + step, 4))
+
+    for core_step in range(2):
+        result(0, other, core_step, 0)
+    for core_step in reversed(range(2)):
+        for mp_step in reversed(range(mp)):
+            result(0, chip, core_step, mp_step)
+
+    arrived(1, 1)
+    arrived(0, 1)
+
+    @pl.loop(0, 2)
+    def _(step):
+        weigh(1, chip * 2 + step)
+
+    for mp_step in range(1, mp):
+        for core_step in range(2):
+            result(0, other, core_step, mp_step)
+
+    arrived(2, 1)
+    for core_step in reversed(range(2)):
+        attend(1, chip * 2 + lax.rem(core + core_step, 2))
+        for mp_step in reversed(range(mp)):
+            result(1, chip, core_step, mp_step)
+
+    whole = kept.at[pl.ds(0, 2)]
+    pltpu.make_async_copy(whole, whole, sent).wait()
+    moved = out.at[:, pl.ds(0, out.shape[1] - 2 * width)]
+    pltpu.make_async_copy(moved, moved, result_out).wait()
+    pltpu.make_async_copy(moved, moved, result_in).wait()
+
+
+def duo_call(query, key, value, clip_lengths):
+    rows, width = query.shape
+    heads = width // HD
+    mp = lax.axis_size("mp")
+    wide = heads // 6
+    dma = pltpu.SemaphoreType.DMA
+    whole = pl.BlockSpec(memory_space=pl.ANY)
+    return pl.pallas_call(
+        functools.partial(duo, heads),
+        out_shape=pltpu.VMEM((rows // mp, width * mp), jnp.bfloat16),
+        in_specs=[whole] * 4,
+        out_specs=pl.BlockSpec(memory_space=pltpu.VMEM),
+        scratch_shapes=[
+            pltpu.VMEM((3, 2, 4 * rows, wide * HD), jnp.bfloat16),
+            pltpu.VMEM((wide, 4 * rows, 4 * rows), jnp.bfloat16),
+            pltpu.VMEM((wide, 4 * rows, HD), jnp.float32),
+            pltpu.VMEM((2, 4 * rows, wide * HD), jnp.bfloat16),
+            pltpu.SMEM(clip_lengths.shape, jnp.int32),
+            dma((3, 2)), dma(()), dma(()), dma(()), dma(()), pltpu.SemaphoreType.REGULAR,
+        ],
+        compiler_params=pltpu.CompilerParams(collective_id=0, has_side_effects=True),
+        name="packed_attention",
+    )(clip_lengths, query, key, value)
+
+
 def shards(query, key, value, clip_lengths):
     rows, width = query.shape
     heads = width // HD
     group = lax.axis_size("seq") // clip_lengths.shape[0]
     mp = lax.axis_size("mp")
+    if group == 4 and heads % 6 == 0 and rows % (16 * mp) == 0 and 1 < mp:
+        return duo_call(query, key, value, clip_lengths)
     pair = 2 if group % 2 == 0 and heads % 2 == 0 else 1
     per_core = heads // pair
     others = group // pair

time: 42.6 us -> 40.6 us (0.953)
  Pallas kernels: 41.5 us -> 39.5 us
    pallas_call x1, Pallas kernels: 41.5 us -> 39.5 us  [duo_call(): pl.pallas_call(functools.partial(duo, heads), out_shape=pltpu.VMEM((rows...]
where the time goes in v1:
time: 40.6 us; the launch traced here: 40.4 us
  Pallas kernels  39.5 us (97%)
  local copies, waits for them, and re-layouts  0.88 us (2%)
    pallas_call x1, Pallas kernels, duo_call(): pl.pallas_call(functools.partial(duo, heads), out_shape=pltpu.VMEM((rows...  39.5 us
    unnamed x1, local copies, waits for them, and re-layouts  0.88 us

profile of v1, /device:TPU:0, one launch (start us, length us, event | category | flops | bytes accessed | tf_op | source)
XLA Modules:
  0.0 40.4 jit_solution(13624840525298521468)
XLA Ops:
  0.0 39.5 %packed_attention.1 = bf16[128,3072]{1,0:T(8,128)(2,1)S(1)} custom-call(s32[4,4]{1,0:T(4,128)} %lengths.1, bf16[256,1536]{1,0:T(8,128)(2,1)} %query.1, bf16[256,1536]{1,0:T(8,128)(2,1)} %key.1, bf16[256,1536]{1,0:T(8,128)(2,1)} %value.1), custom_call_target="tpu_custom_call" | custom-call | tf_op jit(solution)/shard_map/packed_attention/pallas_call | solution.py:450
  39.5 0.9 %copy.6 = bf16[128,3072]{1,0:T(8,128)(2,1)} copy(bf16[128,3072]{1,0:T(8,128)(2,1)S(1)} %packed_attention.1) | data formatting | bytes 1572864

commit v2 on v1

--- a/solution.py
+++ b/solution.py
@@ -256,7 +256,7 @@
 
 
 def duo(
-    heads,
+    heads, pieces,
     lengths, query, key, value, out,
     kept, weights, totals, results, table,
     landed, sent, result_in, result_out, table_in, ready,
@@ -264,9 +264,7 @@
     rows = query.shape[0]
     mp = lax.axis_size("mp")
     part = rows // mp
-    per_core = heads // 2
-    wide = per_core // 3
-    width = wide * HD
+    wide = heads // 4
     slots = lengths.shape[1]
     seq_index = lax.axis_index("seq")
     mp_index = lax.axis_index("mp")
@@ -280,35 +278,33 @@
     def device(there_chip, there_core, there_mp):
         return {"seq": bucket * 4 + there_chip * 2 + there_core, "mp": there_mp}
 
-    def columns(owner, third):
-        return pl.ds(pl.multiple_of(owner * per_core * HD + third * width, width), width)
+    def lanes(piece, base=0):
+        first, count = pieces[piece]
+        return pl.ds(pl.multiple_of((base + first) * HD, HD), count * HD)
 
     def block_at(index):
         return pl.ds(pl.multiple_of(index * rows, rows), rows)
 
-    def send(kind, phase, there_chip, there_core):
-        third = 2 if phase else there_chip
+    def send(kind, piece, there_chip, there_core):
         return pltpu.make_async_remote_copy(
-            src_ref=inputs[kind].at[:, columns(there_core, third)],
-            dst_ref=kept.at[kind, phase, block_at(place), :],
-            send_sem=sent, recv_sem=landed.at[kind, phase],
+            src_ref=inputs[kind].at[:, lanes(piece, (there_core * 2 + there_chip) * wide)],
+            dst_ref=kept.at[kind, block_at(place), lanes(piece)],
+            send_sem=sent, recv_sem=landed.at[kind, piece],
             device_id=device(there_chip, there_core, mp_index), device_id_type=MESH,
         )
 
-    def keep(kind, phase):
-        third = 2 if phase else chip
+    def keep(kind, piece):
         return pltpu.make_async_copy(
-            inputs[kind].at[:, columns(core, third)], kept.at[kind, phase, block_at(place), :], landed.at[kind, phase]
+            inputs[kind].at[:, lanes(piece, (core * 2 + chip) * wide)],
+            kept.at[kind, block_at(place), lanes(piece)], landed.at[kind, piece],
         )
 
-    def result(turn, there_chip, core_step, mp_step):
+    def result(piece, there_chip, core_step, mp_step):
         there_core = lax.rem(core + core_step, 2)
         there_mp = lax.rem(mp_index + mp_step, mp)
         first = (there_chip * 2 + there_core) * rows + there_mp * part
-        source = results.at[turn, pl.ds(pl.multiple_of(first, part), part), :]
-        third = 2 if turn else chip
-        column = (mp_index * heads + core * per_core) * HD + third * width
-        target = out.at[:, pl.ds(pl.multiple_of(column, width), width)]
+        source = results.at[pl.ds(pl.multiple_of(first, part), part), lanes(piece)]
+        target = out.at[:, lanes(piece, mp_index * heads + (core * 2 + chip) * wide)]
         if there_chip is chip and core_step == 0 and mp_step == 0:
             target[...] = source[...]
             return
@@ -330,14 +326,15 @@
     known = len(far) + lax.select(chip == 0, len(beside), 0)
     pl.semaphore_wait(barrier, known)
 
-    for kind, phase in ((1, 0), (0, 0), (2, 0), (1, 1), (2, 1)):
-        for there_core in range(2):
-            send(kind, phase, other, there_core).start()
+    for piece in range(len(pieces)):
+        for kind in (1, 0, 2):
+            for there_core in range(2):
+                send(kind, piece, other, there_core).start()
     fetch = pltpu.make_async_copy(lengths, table, table_in)
     fetch.start()
-    for phase in range(2):
+    for piece in range(len(pieces)):
         for kind in (1, 0, 2):
-            keep(kind, phase).start()
+            keep(kind, piece).start()
 
     greet(ready, far)
 
@@ -349,9 +346,9 @@
 
     pl.when(chip != 0)(lambda: pl.semaphore_wait(ready, 2 * len(far)))
 
-    for phase in range(2):
+    for piece in range(len(pieces)):
         for kind in (1, 0, 2):
-            send(kind, phase, chip, 1 - core).start()
+            send(kind, piece, chip, 1 - core).start()
 
     fetch.wait()
     ends = []
@@ -369,19 +366,20 @@
     k_ids = ids(lax.broadcasted_iota(jnp.int32, (1, 4 * rows), 1))
     factor = LOG2E / HD**0.5
 
-    def arrived(kind, phase):
-        ref = kept.at[kind, phase]
-        if kind == 0 and phase:
-            ref = kept.at[kind, phase, pl.ds(pl.multiple_of(chip * 2 * rows, rows), 2 * rows), :]
-        pltpu.make_async_copy(ref, ref, landed.at[kind, phase]).wait()
-
-    def weigh(phase, index):
+    def arrived(kind, piece):
+        ref = kept.at[kind, :, lanes(piece)]
+        pltpu.make_async_copy(ref, ref, landed.at[kind, piece]).wait()
+
+    def heads_of(piece):
+        first, count = pieces[piece]
+        return [(head, slice(head * HD, (head + 1) * HD)) for head in range(first, first + count)]
+
+    def weigh(piece, index):
         block = block_at(index)
         q_ids = ids(lax.broadcasted_iota(jnp.int32, (rows, 1), 0) + index * rows)
-        for head in range(wide):
-            lanes = slice(head * HD, (head + 1) * HD)
+        for head, lane in heads_of(piece):
             score = lax.dot_general(
-                kept[0, phase, block, lanes], kept[1, phase, :, lanes],
+                kept[0, block, lane], kept[1, :, lane],
                 (((1,), (1,)), ((), ())), preferred_element_type=jnp.float32,
             )
             score = jnp.where(q_ids == k_ids, score, NEG)
@@ -390,52 +388,56 @@
             totals[head, block, :] = jnp.broadcast_to(jnp.sum(weight, axis=1, keepdims=True), (rows, HD))
             weights[head, block, :] = weight.astype(jnp.bfloat16)
 
-    def attend(phase, index):
+    def attend(piece, index):
         block = block_at(index)
-        for head in range(wide):
-            lanes = slice(head * HD, (head + 1) * HD)
-            summed = jnp.dot(weights[head, block, :], kept[2, phase, :, lanes], preferred_element_type=jnp.float32)
-            results[phase, block, lanes] = (summed / totals[head, block, :]).astype(jnp.bfloat16)
-
-    arrived(1, 0)
-    arrived(0, 0)
-
-    @pl.loop(0, 4)
-    def _(step):
-        weigh(0, lax.rem(other * 2 + step, 4))
-
-    arrived(2, 0)
-
-    @pl.loop(0, 4)
-    def _(step):
-        attend(0, lax.rem(other * 2 + step, 4))
-
-    for core_step in range(2):
-        result(0, other, core_step, 0)
-    for core_step in reversed(range(2)):
-        for mp_step in reversed(range(mp)):
-            result(0, chip, core_step, mp_step)
-
-    arrived(1, 1)
-    arrived(0, 1)
-
-    @pl.loop(0, 2)
-    def _(step):
-        weigh(1, chip * 2 + step)
-
-    for mp_step in range(1, mp):
+        for head, lane in heads_of(piece):
+            summed = jnp.dot(weights[head, block, :], kept[2, :, lane], preferred_element_type=jnp.float32)
+            results[block, lane] = (summed / totals[head, block, :]).astype(jnp.bfloat16)
+
+    def direct(piece):
         for core_step in range(2):
-            result(0, other, core_step, mp_step)
-
-    arrived(2, 1)
-    for core_step in reversed(range(2)):
-        attend(1, chip * 2 + lax.rem(core + core_step, 2))
-        for mp_step in reversed(range(mp)):
-            result(1, chip, core_step, mp_step)
-
-    whole = kept.at[pl.ds(0, 2)]
+            result(piece, other, core_step, 0)
+
+    def diagonal(piece):
+        for mp_step in range(1, mp):
+            for core_step in range(2):
+                result(piece, other, core_step, mp_step)
+
+    def own(piece):
+        for core_step in reversed(range(2)):
+            for mp_step in reversed(range(mp)):
+                result(piece, chip, core_step, mp_step)
+
+    for piece in range(len(pieces)):
+        last = piece == len(pieces) - 1
+        arrived(1, piece)
+        arrived(0, piece)
+
+        @pl.loop(0, 4)
+        def _(step):
+            weigh(piece, lax.rem(other * 2 + step, 4))
+
+        arrived(2, piece)
+        if last:
+            diagonal(piece - 1)
+
+        @pl.loop(0, 2)
+        def _(step):
+            attend(piece, other * 2 + step)
+
+        if last:
+            diagonal(piece)
+        direct(piece)
+
+        @pl.loop(0, 2)
+        def _(step):
+            attend(piece, chip * 2 + step)
+
+        own(piece)
+
+    whole = kept.at[:, pl.ds(0, 3 * rows)]
     pltpu.make_async_copy(whole, whole, sent).wait()
-    moved = out.at[:, pl.ds(0, out.shape[1] - 2 * width)]
+    moved = out.at[:, pl.ds(0, out.shape[1] - wide * HD)]
     pltpu.make_async_copy(moved, moved, result_out).wait()
     pltpu.make_async_copy(moved, moved, result_in).wait()
 
@@ -444,21 +446,23 @@
     rows, width = query.shape
     heads = width // HD
     mp = lax.axis_size("mp")
-    wide = heads // 6
+    wide = heads // 4
+    early = (wide + 1) // 2
+    pieces = [(0, early)] + [(head, 1) for head in range(early, wide)]
     dma = pltpu.SemaphoreType.DMA
     whole = pl.BlockSpec(memory_space=pl.ANY)
     return pl.pallas_call(
-        functools.partial(duo, heads),
+        functools.partial(duo, heads, pieces),
         out_shape=pltpu.VMEM((rows // mp, width * mp), jnp.bfloat16),
         in_specs=[whole] * 4,
         out_specs=pl.BlockSpec(memory_space=pltpu.VMEM),
         scratch_shapes=[
-            pltpu.VMEM((3, 2, 4 * rows, wide * HD), jnp.bfloat16),
+            pltpu.VMEM((3, 4 * rows, wide * HD), jnp.bfloat16),
             pltpu.VMEM((wide, 4 * rows, 4 * rows), jnp.bfloat16),
             pltpu.VMEM((wide, 4 * rows, HD), jnp.float32),
-            pltpu.VMEM((2, 4 * rows, wide * HD), jnp.bfloat16),
+            pltpu.VMEM((4 * rows, wide * HD), jnp.bfloat16),
             pltpu.SMEM(clip_lengths.shape, jnp.int32),
-            dma((3, 2)), dma(()), dma(()), dma(()), dma(()), pltpu.SemaphoreType.REGULAR,
+            dma((3, len(pieces))), dma(()), dma(()), dma(()), dma(()), pltpu.SemaphoreType.REGULAR,
         ],
         compiler_params=pltpu.CompilerParams(collective_id=0, has_side_effects=True),
         name="packed_attention",
@@ -470,7 +474,7 @@
     heads = width // HD
     group = lax.axis_size("seq") // clip_lengths.shape[0]
     mp = lax.axis_size("mp")
-    if group == 4 and heads % 6 == 0 and rows % (16 * mp) == 0 and 1 < mp:
+    if group == 4 and heads % 4 == 0 and rows % (16 * mp) == 0 and mp > 1:
         return duo_call(query, key, value, clip_lengths)
     pair = 2 if group % 2 == 0 and heads % 2 == 0 else 1
     per_core = heads // pair

time: 40.6 us -> 39.5 us (0.973)
  Pallas kernels: 39.5 us -> 38.5 us
    pallas_call x1, Pallas kernels: 39.5 us -> 38.5 us  [duo_call(): pl.pallas_call(functools.partial(duo, heads, pieces), out_shape=pltpu.VME...]
where the time goes in v2:
time: 39.5 us; the launch traced here: 39.4 us
  Pallas kernels  38.5 us (97%)
  local copies, waits for them, and re-layouts  0.88 us (2%)
    pallas_call x1, Pallas kernels, duo_call(): pl.pallas_call(functools.partial(duo, heads, pieces), out_shape=pltpu.VME...  38.5 us
    unnamed x1, local copies, waits for them, and re-layouts  0.88 us

profile of v2, /device:TPU:0, one launch (start us, length us, event | category | flops | bytes accessed | tf_op | source)
XLA Modules:
  0.0 39.4 jit_solution(2316223055450521127)
XLA Ops:
  0.0 38.5 %packed_attention.1 = bf16[128,3072]{1,0:T(8,128)(2,1)S(1)} custom-call(s32[4,4]{1,0:T(4,128)} %lengths.1, bf16[256,1536]{1,0:T(8,128)(2,1)} %query.1, bf16[256,1536]{1,0:T(8,128)(2,1)} %key.1, bf16[256,1536]{1,0:T(8,128)(2,1)} %value.1), custom_call_target="tpu_custom_call" | custom-call | tf_op jit(solution)/shard_map/packed_attention/pallas_call | solution.py:454
  38.5 0.9 %copy.6 = bf16[128,3072]{1,0:T(8,128)(2,1)} copy(bf16[128,3072]{1,0:T(8,128)(2,1)S(1)} %packed_attention.1) | data formatting | bytes 1572864

commit v3 on v2

--- a/solution.py
+++ b/solution.py
@@ -300,7 +300,7 @@
         )
 
     def result(piece, there_chip, core_step, mp_step):
-        there_core = lax.rem(core + core_step, 2)
+        there_core = core_step if there_chip is other else lax.rem(core + core_step, 2)
         there_mp = lax.rem(mp_index + mp_step, mp)
         first = (there_chip * 2 + there_core) * rows + there_mp * part
         source = results.at[pl.ds(pl.multiple_of(first, part), part), lanes(piece)]
@@ -408,31 +408,28 @@
             for mp_step in reversed(range(mp)):
                 result(piece, chip, core_step, mp_step)
 
+    def each(work, piece, there_chip):
+        @pl.loop(0, 2)
+        def _(step):
+            work(piece, there_chip * 2 + step)
+
+    last = len(pieces) - 1
     for piece in range(len(pieces)):
-        last = piece == len(pieces) - 1
         arrived(1, piece)
         arrived(0, piece)
-
-        @pl.loop(0, 4)
-        def _(step):
-            weigh(piece, lax.rem(other * 2 + step, 4))
-
+        each(weigh, piece, other)
+        if piece < last:
+            each(weigh, piece, chip)
         arrived(2, piece)
-        if last:
+        if piece:
             diagonal(piece - 1)
-
-        @pl.loop(0, 2)
-        def _(step):
-            attend(piece, other * 2 + step)
-
-        if last:
+        each(attend, piece, other)
+        if piece == last:
             diagonal(piece)
         direct(piece)
-
-        @pl.loop(0, 2)
-        def _(step):
-            attend(piece, chip * 2 + step)
-
+        if piece == last:
+            each(weigh, piece, chip)
+        each(attend, piece, chip)
         own(piece)
 
     whole = kept.at[:, pl.ds(0, 3 * rows)]

time: 39.5 us -> 39 us (0.987)
  Pallas kernels: 38.5 us -> 38 us
    pallas_call x1, Pallas kernels: 38.5 us -> 38 us  [duo_call(): pl.pallas_call(functools.partial(duo, heads, pieces), out_shape=pltpu.VME...]
where the time goes in v3:
time: 39 us; the launch traced here: 38.8 us
  Pallas kernels  38 us (97%)
  local copies, waits for them, and re-layouts  0.88 us (2%)
    pallas_call x1, Pallas kernels, duo_call(): pl.pallas_call(functools.partial(duo, heads, pieces), out_shape=pltpu.VME...  38 us
    unnamed x1, local copies, waits for them, and re-layouts  0.88 us

profile of v3, /device:TPU:0, one launch (start us, length us, event | category | flops | bytes accessed | tf_op | source)
XLA Modules:
  0.0 38.8 jit_solution(17344301476015780670)
XLA Ops:
  0.0 38.0 %packed_attention.1 = bf16[128,3072]{1,0:T(8,128)(2,1)S(1)} custom-call(s32[4,4]{1,0:T(4,128)} %lengths.1, bf16[256,1536]{1,0:T(8,128)(2,1)} %query.1, bf16[256,1536]{1,0:T(8,128)(2,1)} %key.1, bf16[256,1536]{1,0:T(8,128)(2,1)} %value.1), custom_call_target="tpu_custom_call" | custom-call | tf_op jit(solution)/shard_map/packed_attention/pallas_call | solution.py:451
  38.0 0.9 %copy.6 = bf16[128,3072]{1,0:T(8,128)(2,1)} copy(bf16[128,3072]{1,0:T(8,128)(2,1)S(1)} %packed_attention.1) | data formatting | bytes 1572864

commit v4 on v3

--- a/solution.py
+++ b/solution.py
@@ -388,8 +388,8 @@
             totals[head, block, :] = jnp.broadcast_to(jnp.sum(weight, axis=1, keepdims=True), (rows, HD))
             weights[head, block, :] = weight.astype(jnp.bfloat16)
 
-    def attend(piece, index):
-        block = block_at(index)
+    def attend(piece, index, count=1):
+        block = pl.ds(pl.multiple_of(index * count * rows, count * rows), count * rows)
         for head, lane in heads_of(piece):
             summed = jnp.dot(weights[head, block, :], kept[2, :, lane], preferred_element_type=jnp.float32)
             results[block, lane] = (summed / totals[head, block, :]).astype(jnp.bfloat16)
@@ -423,7 +423,10 @@
         arrived(2, piece)
         if piece:
             diagonal(piece - 1)
-        each(attend, piece, other)
+        if piece == last:
+            attend(piece, other, 2)
+        else:
+            each(attend, piece, other)
         if piece == last:
             diagonal(piece)
         direct(piece)

time: 39 us -> 38.7 us (level)
  no operation moved by 1% of the time
where the time goes in v4:
time: 38.7 us; the launch traced here: 38.6 us
  Pallas kernels  37.7 us (97%)
  local copies, waits for them, and re-layouts  0.88 us (2%)
    pallas_call x1, Pallas kernels, duo_call(): pl.pallas_call(functools.partial(duo, heads, pieces), out_shape=pltpu.VME...  37.7 us
    unnamed x1, local copies, waits for them, and re-layouts  0.88 us

profile of v4, /device:TPU:0, one launch (start us, length us, event | category | flops | bytes accessed | tf_op | source)
XLA Modules:
  0.0 38.6 jit_solution(16200740440254686093)
XLA Ops:
  0.0 37.7 %packed_attention.1 = bf16[128,3072]{1,0:T(8,128)(2,1)S(1)} custom-call(s32[4,4]{1,0:T(4,128)} %lengths.1, bf16[256,1536]{1,0:T(8,128)(2,1)} %query.1, bf16[256,1536]{1,0:T(8,128)(2,1)} %key.1, bf16[256,1536]{1,0:T(8,128)(2,1)} %value.1), custom_call_target="tpu_custom_call" | custom-call | tf_op jit(solution)/shard_map/packed_attention/pallas_call | solution.py:454
  37.7 0.9 %copy.6 = bf16[128,3072]{1,0:T(8,128)(2,1)} copy(bf16[128,3072]{1,0:T(8,128)(2,1)S(1)} %packed_attention.1) | data formatting | bytes 1572864

commit v5 on v4

--- a/solution.py
+++ b/solution.py
@@ -398,9 +398,9 @@
         for core_step in range(2):
             result(piece, other, core_step, 0)
 
-    def diagonal(piece):
+    def diagonal(piece, cores=(0, 1)):
         for mp_step in range(1, mp):
-            for core_step in range(2):
+            for core_step in cores:
                 result(piece, other, core_step, mp_step)
 
     def own(piece):
@@ -420,9 +420,14 @@
         each(weigh, piece, other)
         if piece < last:
             each(weigh, piece, chip)
+        if piece:
+            both = jnp.logical_and(mp_index == 1, chip == 1)
+            pl.when(mp_index == 1)(lambda: diagonal(piece - 1, (0,)))
+            pl.when(both)(lambda: diagonal(piece - 1, (1,)))
         arrived(2, piece)
         if piece:
-            diagonal(piece - 1)
+            pl.when(mp_index != 1)(lambda: diagonal(piece - 1, (0,)))
+            pl.when(jnp.logical_not(both))(lambda: diagonal(piece - 1, (1,)))
         if piece == last:
             attend(piece, other, 2)
         else:

time: 38.7 us -> 38.6 us (level)
  no operation moved by 1% of the time
where the time goes in v5:
time: 38.6 us; the launch traced here: 38.4 us
  Pallas kernels  37.5 us (97%)
  local copies, waits for them, and re-layouts  0.88 us (2%)
    pallas_call x1, Pallas kernels, duo_call(): pl.pallas_call(functools.partial(duo, heads, pieces), out_shape=pltpu.VME...  37.5 us
    unnamed x1, local copies, waits for them, and re-layouts  0.88 us

profile of v5, /device:TPU:0, one launch (start us, length us, event | category | flops | bytes accessed | tf_op | source)
XLA Modules:
  0.0 38.4 jit_solution(5528643213628161458)
XLA Ops:
  0.0 37.5 %packed_attention.1 = bf16[128,3072]{1,0:T(8,128)(2,1)S(1)} custom-call(s32[4,4]{1,0:T(4,128)} %lengths.1, bf16[256,1536]{1,0:T(8,128)(2,1)} %query.1, bf16[256,1536]{1,0:T(8,128)(2,1)} %key.1, bf16[256,1536]{1,0:T(8,128)(2,1)} %value.1), custom_call_target="tpu_custom_call" | custom-call | tf_op jit(solution)/shard_map/packed_attention/pallas_call | solution.py:459
  37.5 0.9 %copy.6 = bf16[128,3072]{1,0:T(8,128)(2,1)} copy(bf16[128,3072]{1,0:T(8,128)(2,1)S(1)} %packed_attention.1) | data formatting | bytes 1572864

commit v6 on v5

--- a/solution.py
+++ b/solution.py
@@ -322,9 +322,11 @@
             pl.semaphore_signal(semaphore, inc=1, device_id=there, device_id_type=MESH)
 
     greet(barrier, far)
-    pl.when(chip == 0)(lambda: greet(barrier, beside))
-    known = len(far) + lax.select(chip == 0, len(beside), 0)
-    pl.semaphore_wait(barrier, known)
+    root = jnp.logical_and(chip == 0, mp_index == 0)
+    leaf = jnp.logical_and(chip == 0, mp_index != 0)
+    rooted = [device(0, b, 0) for b in range(2)]
+    pl.when(root)(lambda: greet(barrier, beside))
+    pl.semaphore_wait(barrier, len(far) + lax.select(leaf, len(rooted), 0))
 
     for piece in range(len(pieces)):
         for kind in (1, 0, 2):
@@ -338,11 +340,15 @@
 
     greet(ready, far)
 
-    @pl.when(chip == 0)
+    pl.when(leaf)(lambda: greet(ready, rooted))
+
+    @pl.when(root)
     def _():
+        pl.semaphore_wait(ready, len(far) + len(beside))
         greet(ready, beside)
-        pl.semaphore_wait(ready, len(far) + len(beside))
-        greet(ready, far)
+
+    pl.when(leaf)(lambda: pl.semaphore_wait(ready, len(far) + len(rooted)))
+    pl.when(chip == 0)(lambda: greet(ready, far))
 
     pl.when(chip != 0)(lambda: pl.semaphore_wait(ready, 2 * len(far)))
 
@@ -424,6 +430,8 @@
             both = jnp.logical_and(mp_index == 1, chip == 1)
             pl.when(mp_index == 1)(lambda: diagonal(piece - 1, (0,)))
             pl.when(both)(lambda: diagonal(piece - 1, (1,)))
+        if piece == last:
+            each(weigh, piece, chip)
         arrived(2, piece)
         if piece:
             pl.when(mp_index != 1)(lambda: diagonal(piece - 1, (0,)))
@@ -435,8 +443,6 @@
         if piece == last:
             diagonal(piece)
         direct(piece)
-        if piece == last:
-            each(weigh, piece, chip)
         each(attend, piece, chip)
         own(piece)
 

time: 38.6 us -> 38.6 us (level)
  no operation moved by 1% of the time
where the time goes in v6:
time: 38.6 us; the launch traced here: 38.4 us
  Pallas kernels  37.5 us (97%)
  local copies, waits for them, and re-layouts  0.88 us (2%)
    pallas_call x1, Pallas kernels, duo_call(): pl.pallas_call(functools.partial(duo, heads, pieces), out_shape=pltpu.VME...  37.5 us
    unnamed x1, local copies, waits for them, and re-layouts  0.88 us

profile of v6, /device:TPU:0, one launch (start us, length us, event | category | flops | bytes accessed | tf_op | source)
XLA Modules:
  0.0 38.4 jit_solution(10229942573211118460)
XLA Ops:
  0.0 37.5 %packed_attention.1 = bf16[128,3072]{1,0:T(8,128)(2,1)S(1)} custom-call(s32[4,4]{1,0:T(4,128)} %lengths.1, bf16[256,1536]{1,0:T(8,128)(2,1)} %query.1, bf16[256,1536]{1,0:T(8,128)(2,1)} %key.1, bf16[256,1536]{1,0:T(8,128)(2,1)} %value.1), custom_call_target="tpu_custom_call" | custom-call | tf_op jit(solution)/shard_map/packed_attention/pallas_call | solution.py:465
  37.5 0.9 %copy.6 = bf16[128,3072]{1,0:T(8,128)(2,1)} copy(bf16[128,3072]{1,0:T(8,128)(2,1)S(1)} %packed_attention.1) | data formatting | bytes 1572864

commit v7 on v6

--- a/solution.py
+++ b/solution.py
@@ -259,7 +259,7 @@
     heads, pieces,
     lengths, query, key, value, out,
     kept, weights, totals, results, table,
-    landed, sent, result_in, result_out, table_in, ready,
+    landed, sent, result_in, table_in, ready,
 ):
     rows = query.shape[0]
     mp = lax.axis_size("mp")
@@ -289,14 +289,14 @@
         return pltpu.make_async_remote_copy(
             src_ref=inputs[kind].at[:, lanes(piece, (there_core * 2 + there_chip) * wide)],
             dst_ref=kept.at[kind, block_at(place), lanes(piece)],
-            send_sem=sent, recv_sem=landed.at[kind, piece],
+            send_sem=sent, recv_sem=landed.at[kind // 2, piece],
             device_id=device(there_chip, there_core, mp_index), device_id_type=MESH,
         )
 
     def keep(kind, piece):
         return pltpu.make_async_copy(
             inputs[kind].at[:, lanes(piece, (core * 2 + chip) * wide)],
-            kept.at[kind, block_at(place), lanes(piece)], landed.at[kind, piece],
+            kept.at[kind, block_at(place), lanes(piece)], landed.at[kind // 2, piece],
         )
 
     def result(piece, there_chip, core_step, mp_step):
@@ -309,7 +309,7 @@
             target[...] = source[...]
             return
         pltpu.make_async_remote_copy(
-            src_ref=source, dst_ref=target, send_sem=result_out, recv_sem=result_in,
+            src_ref=source, dst_ref=target, send_sem=sent, recv_sem=result_in,
             device_id=device(there_chip, there_core, there_mp), device_id_type=MESH,
         ).start()
 
@@ -373,8 +373,8 @@
     factor = LOG2E / HD**0.5
 
     def arrived(kind, piece):
-        ref = kept.at[kind, :, lanes(piece)]
-        pltpu.make_async_copy(ref, ref, landed.at[kind, piece]).wait()
+        ref = kept.at[2 if kind == 2 else pl.ds(0, 2), :, lanes(piece)]
+        pltpu.make_async_copy(ref, ref, landed.at[kind // 2, piece]).wait()
 
     def heads_of(piece):
         first, count = pieces[piece]
@@ -421,7 +421,6 @@
 
     last = len(pieces) - 1
     for piece in range(len(pieces)):
-        arrived(1, piece)
         arrived(0, piece)
         each(weigh, piece, other)
         if piece < last:
@@ -440,16 +439,16 @@
             attend(piece, other, 2)
         else:
             each(attend, piece, other)
+        direct(piece)
         if piece == last:
             diagonal(piece)
-        direct(piece)
         each(attend, piece, chip)
         own(piece)
 
     whole = kept.at[:, pl.ds(0, 3 * rows)]
     pltpu.make_async_copy(whole, whole, sent).wait()
     moved = out.at[:, pl.ds(0, out.shape[1] - wide * HD)]
-    pltpu.make_async_copy(moved, moved, result_out).wait()
+    pltpu.make_async_copy(moved, moved, sent).wait()
     pltpu.make_async_copy(moved, moved, result_in).wait()
 
 
@@ -473,7 +472,7 @@
             pltpu.VMEM((wide, 4 * rows, HD), jnp.float32),
             pltpu.VMEM((4 * rows, wide * HD), jnp.bfloat16),
             pltpu.SMEM(clip_lengths.shape, jnp.int32),
-            dma((3, len(pieces))), dma(()), dma(()), dma(()), dma(()), pltpu.SemaphoreType.REGULAR,
+            dma((2, len(pieces))), dma(()), dma(()), dma(()), pltpu.SemaphoreType.REGULAR,
         ],
         compiler_params=pltpu.CompilerParams(collective_id=0, has_side_effects=True),
         name="packed_attention",

time: 38.6 us -> 38.5 us (level)
  no operation moved by 1% of the time
where the time goes in v7:
time: 38.5 us; the launch traced here: 38.4 us
  Pallas kernels  37.5 us (97%)
  local copies, waits for them, and re-layouts  0.88 us (2%)
    pallas_call x1, Pallas kernels, duo_call(): pl.pallas_call(functools.partial(duo, heads, pieces), out_shape=pltpu.VME...  37.5 us
    unnamed x1, local copies, waits for them, and re-layouts  0.88 us

profile of v7, /device:TPU:0, one launch (start us, length us, event | category | flops | bytes accessed | tf_op | source)
XLA Modules:
  0.0 38.4 jit_solution(3724856318919226600)
XLA Ops:
  0.0 37.5 %packed_attention.1 = bf16[128,3072]{1,0:T(8,128)(2,1)S(1)} custom-call(s32[4,4]{1,0:T(4,128)} %lengths.1, bf16[256,1536]{1,0:T(8,128)(2,1)} %query.1, bf16[256,1536]{1,0:T(8,128)(2,1)} %key.1, bf16[256,1536]{1,0:T(8,128)(2,1)} %value.1), custom_call_target="tpu_custom_call" | custom-call | tf_op jit(solution)/shard_map/packed_attention/pallas_call | solution.py:464
  37.5 0.9 %copy.6 = bf16[128,3072]{1,0:T(8,128)(2,1)} copy(bf16[128,3072]{1,0:T(8,128)(2,1)S(1)} %packed_attention.1) | data formatting | bytes 1572864

commit v8 on v6

--- a/solution.py
+++ b/solution.py
@@ -440,9 +440,9 @@
             attend(piece, other, 2)
         else:
             each(attend, piece, other)
+        direct(piece)
         if piece == last:
             diagonal(piece)
-        direct(piece)
         each(attend, piece, chip)
         own(piece)
 

time: 38.6 us -> 38.6 us (level)
  no operation moved by 1% of the time
where the time goes in v8:
time: 38.6 us; the launch traced here: 38.4 us
  Pallas kernels  37.5 us (97%)
  local copies, waits for them, and re-layouts  0.88 us (2%)
    pallas_call x1, Pallas kernels, duo_call(): pl.pallas_call(functools.partial(duo, heads, pieces), out_shape=pltpu.VME...  37.5 us
    unnamed x1, local copies, waits for them, and re-layouts  0.88 us

profile of v8, /device:TPU:0, one launch (start us, length us, event | category | flops | bytes accessed | tf_op | source)
XLA Modules:
  0.0 38.4 jit_solution(5643195875188618414)
XLA Ops:
  0.0 37.5 %packed_attention.1 = bf16[128,3072]{1,0:T(8,128)(2,1)S(1)} custom-call(s32[4,4]{1,0:T(4,128)} %lengths.1, bf16[256,1536]{1,0:T(8,128)(2,1)} %query.1, bf16[256,1536]{1,0:T(8,128)(2,1)} %key.1, bf16[256,1536]{1,0:T(8,128)(2,1)} %value.1), custom_call_target="tpu_custom_call" | custom-call | tf_op jit(solution)/shard_map/packed_attention/pallas_call | solution.py:465
  37.5 0.9 %copy.6 = bf16[128,3072]{1,0:T(8,128)(2,1)} copy(bf16[128,3072]{1,0:T(8,128)(2,1)S(1)} %packed_attention.1) | data formatting | bytes 1572864
